TPU v7x, 32 devices: a whole 2x2x4 slice. The times are simulated.
32 devices in a mesh: seq: 8 (over z, x), tensor: 4 (over y, core).
Axes of the slice: x: 2, y: 2, z: 4, core: 2. Of those that a mesh axis runs over, the one named last changes fastest.
Arguments:
- hidden_in: bfloat16 [16, 5120], replicated, may hold values from -6 to 6
- united_down: bfloat16 [5120, 2112], P(None, 'tensor'), may hold values from -0.078125 to 0.078125
- q_gain: float32 [1536], replicated, may hold values from 0.1 to 1.9
- kv_gain: float32 [512], replicated, may hold values from 0.1 to 1.9
- q_up: bfloat16 [1536, 24576], P('seq', 'tensor'), may hold values from -0.15625 to 0.15625
- key_up: bfloat16 [512, 16384], P(None, 'tensor'), may hold values from -0.25 to 0.25
- value_up: bfloat16 [512, 16384], P(None, 'tensor'), may hold values from -0.0625 to 0.0625
- latent_block_store: bfloat16 [512, 128, 512], P(('seq', 'tensor')), may hold values from -24 to 24
- rope_pool: bfloat16 [512, 64, 128], P(('seq', 'tensor')), may hold values from -124 to 124
- lengths: int32 [16], replicated, may hold values from 2048 to 4096, as said below
- block_table: int32 [16, 32], P(None, 'seq'), may hold values from 0 to 511, as said below
Outputs:
- attn_out: bfloat16 [16, 16384], P(None, 'tensor')
- new_entry: bfloat16 [16, 576], replicated
Inputs may be any that keep to these rules, and one draw needn't show every extreme that they name: `lengths`: every sequence holds 2048 to 4096 cached positions; one sequence holds exactly 4096 and another exactly 2048. block_table[b, j] is the pool slot of positions j * 128 to (j + 1) * 128 - 1 of sequence b. The columns j with j // 4 = s name exactly the 64 slots s * 16 * 4 to (s + 1) * 16 * 4 - 1, each once, in any order; blocks past a sequence's length also name such slots.
All inputs are finite; a program needn't handle non-finite values.
Results may differ from a plain program's by a relative error of at most 0.015.
The roundings to bfloat16 on the way count: a program that leaves them out, or rounds other values in their place, can miss the bound.
Values may be sent and summed in bfloat16 or wider, within the bound.
A program may use at most 128 MiB of HBM per device.

v0:
```python
import jax
import jax.numpy as jnp
from jax import lax
from jax.sharding import PartitionSpec as P

QR = 1536
LATENT_RANK = 512
NOPE = 128
VD = 128
B = 16
BLOCK_POSITIONS = 128
QH = 192


NORM_FLOOR = 1.0
FLOOR_SCORE = -1e30


def rms_scale(row_values, gain_row):
    mean_square = jnp.mean(row_values * row_values, axis=-1, keepdims=True)
    return row_values * lax.rsqrt(mean_square + NORM_FLOOR) * gain_row


def rotate_pairs(rope_pairs, positions):
    half_dim = rope_pairs.shape[-1] // 2
    inverse_freq = 10000.0 ** (
        -2.0 * jnp.arange(half_dim, dtype=jnp.float32) / rope_pairs.shape[-1]
    )
    angles = positions[..., None] * inverse_freq
    cosine = jnp.cos(angles)
    sine_part = jnp.sin(angles)
    front_half = rope_pairs[..., :half_dim]
    back_half = rope_pairs[..., half_dim:]
    return jnp.concatenate(
        [front_half * cosine - back_half * sine_part, front_half * sine_part + back_half * cosine],
        axis=-1,
    )


def attend_slots(query_pack, latent_blocks, rope_blocks, slot_ids, table_flat, base_flat, lengths):
    sequences = query_pack.shape[0]
    span_blocks = table_flat.shape[0] // sequences
    block_rows = latent_blocks.shape[1]
    latent_width = latent_blocks.shape[2]
    flat_index = jnp.arange(table_flat.shape[0], dtype=jnp.int32)
    matches = table_flat[None, :] == slot_ids[:, None]
    owner_seq = jnp.sum(jnp.where(matches, (flat_index // span_blocks)[None, :], 0), axis=1)
    owner_base = jnp.sum(jnp.where(matches, base_flat[None, :], 0), axis=1)
    seq_hot = owner_seq[:, None] == jnp.arange(sequences, dtype=jnp.int32)[None, :]
    picked = jnp.einsum(
        "kb,bhc->khc", seq_hot.astype(jnp.bfloat16), query_pack, preferred_element_type=jnp.float32
    ).astype(jnp.bfloat16)
    scores = jnp.einsum(
        "khc,kpc->khp",
        picked[:, :, :latent_width],
        latent_blocks,
        preferred_element_type=jnp.float32,
    )
    scores = scores + jnp.einsum(
        "khr,krp->khp", picked[:, :, latent_width:], rope_blocks, preferred_element_type=jnp.float32
    )
    limits = jnp.sum(jnp.where(seq_hot, lengths[None, :], 0), axis=1)
    valid_mask = (
        owner_base[:, None] + jnp.arange(block_rows, dtype=jnp.int32)[None, :] < limits[:, None]
    )
    scores = jnp.where(valid_mask[:, None, :], scores, FLOOR_SCORE)
    slot_top = jnp.max(scores, axis=2)
    weights = jnp.where(valid_mask[:, None, :], jnp.exp(scores - slot_top[:, :, None]), 0.0)
    slot_total = jnp.sum(weights, axis=2)
    slot_mixed = jnp.einsum(
        "khp,kpc->khc",
        weights.astype(jnp.bfloat16),
        latent_blocks,
        preferred_element_type=jnp.float32,
    )
    seq_top = jnp.max(jnp.where(seq_hot[:, :, None], slot_top[:, None, :], FLOOR_SCORE), axis=0)
    top_at = jnp.sum(jnp.where(seq_hot[:, :, None], seq_top[None, :, :], 0.0), axis=1)
    factor = jnp.exp(slot_top - top_at)
    hot_wide = seq_hot.astype(jnp.float32)
    seq_total = jnp.einsum(
        "kb,kh->bh", hot_wide, slot_total * factor, precision=lax.Precision.HIGHEST
    )
    seq_mixed = jnp.einsum(
        "kb,khc->bhc", hot_wide, slot_mixed * factor[:, :, None], precision=lax.Precision.HIGHEST
    )
    return (seq_top, seq_total, seq_mixed)


def combine_parts(earlier, later):
    top_one, total_one, mixed_one = earlier
    top_two, total_two, mixed_two = later
    top_both = jnp.maximum(top_one, top_two)
    scale_two = jnp.exp(top_two - top_both)
    return (top_both, total_two * scale_two, mixed_two * scale_two[:, :, None])


def body(
    hidden_in,
    united_down,
    q_gain,
    kv_gain,
    q_up,
    key_up,
    value_up,
    latent_block_store,
    rope_pool,
    lengths,
    block_table,
):
    local_heads = key_up.shape[1] // NOPE
    span_blocks = block_table.shape[1]
    seq_index = lax.axis_index("seq")
    part_cols = jnp.dot(hidden_in, united_down, preferred_element_type=jnp.float32).astype(
        jnp.bfloat16
    )
    united_wide = lax.all_gather(part_cols, "tensor", axis=1, tiled=True).astype(jnp.float32)
    positions = lengths.astype(jnp.float32)
    query_latent = rms_scale(united_wide[:, :QR], q_gain).astype(jnp.bfloat16)
    new_latent = rms_scale(united_wide[:, QR : QR + LATENT_RANK], kv_gain).astype(jnp.bfloat16)
    new_rope = rotate_pairs(united_wide[:, QR + LATENT_RANK :], positions).astype(jnp.bfloat16)
    new_entry = jnp.concatenate([new_latent, new_rope], axis=1)
    row_count = q_up.shape[0]
    own_rows = lax.dynamic_slice_in_dim(query_latent, seq_index * row_count, row_count, 1)
    partial_query = jnp.dot(own_rows, q_up, preferred_element_type=jnp.float32)
    query_full = lax.psum(partial_query, "seq").reshape(B, local_heads, QH)
    query_nope = query_full[:, :, :NOPE].astype(jnp.bfloat16)
    key_heads = key_up.reshape(LATENT_RANK, local_heads, NOPE)
    score_scale = QH ** (-0.5)
    absorbed = jnp.einsum("bhn,khn->bhk", query_nope, key_heads, preferred_element_type=jnp.float32)
    query_lat = (absorbed * score_scale).astype(jnp.bfloat16)
    query_rot = (rotate_pairs(query_full[:, :, NOPE:], positions[:, None]) * score_scale).astype(
        jnp.bfloat16
    )
    query_pack = jnp.concatenate([query_lat, query_rot], axis=2)
    table_flat = block_table.reshape(-1)
    flat_index = jnp.arange(table_flat.shape[0], dtype=jnp.int32)
    base_flat = (seq_index * span_blocks + flat_index % span_blocks) * BLOCK_POSITIONS
    group_base = seq_index * (B * span_blocks)
    initial = (
        jnp.full((B, local_heads), FLOOR_SCORE, jnp.float32),
        jnp.zeros((B, local_heads), jnp.float32),
        jnp.zeros((B, local_heads, LATENT_RANK), jnp.float32),
    )
    latent_piece = lax.all_gather(latent_block_store, "tensor", axis=0, tiled=True)
    rope_piece = lax.all_gather(rope_pool, "tensor", axis=0, tiled=True)
    slot_ids = group_base + jnp.arange(latent_piece.shape[0], dtype=jnp.int32)
    fresh = attend_slots(
        query_pack, latent_piece, rope_piece, slot_ids, table_flat, base_flat, lengths
    )
    top_part, total_part, mixed_part = combine_parts(initial, fresh)
    grand_top = lax.pmax(top_part, "seq")
    factor = jnp.exp(top_part - grand_top)
    total_part, mixed_part = lax.psum((total_part * factor, mixed_part * factor[:, :, None]), "seq")
    top_part = grand_top
    own_score = jnp.sum(
        query_lat.astype(jnp.float32) * new_latent.astype(jnp.float32)[:, None, :], axis=2
    )
    own_score = own_score + jnp.sum(
        query_rot.astype(jnp.float32) * new_rope.astype(jnp.float32)[:, None, :], axis=2
    )
    final_top = jnp.maximum(top_part, own_score)
    old_scale = jnp.exp(top_part - final_top)
    own_weight = jnp.exp(own_score - final_top)
    totals = total_part * old_scale + own_weight
    mixture = mixed_part * old_scale[:, :, None]
    mixture = (
        mixture
        + own_weight.astype(jnp.bfloat16).astype(jnp.float32)[:, :, None]
        * new_latent.astype(jnp.float32)[:, None, :]
    )
    attended = (mixture / totals[:, :, None]).astype(jnp.bfloat16)
    value_heads = value_up.reshape(LATENT_RANK, local_heads, VD)
    attn_out = jnp.einsum("bhk,khv->bhv", attended, value_heads, preferred_element_type=jnp.float32)
    attn_out = attn_out.reshape(B, local_heads * VD).astype(jnp.bfloat16)
    return (attn_out, new_entry)


def solution(mesh):
    in_specs = (
        P(),
        P(None, "tensor"),
        P(),
        P(),
        P("seq", "tensor"),
        P(None, "tensor"),
        P(None, "tensor"),
        P(("seq", "tensor"), None, None),
        P(("seq", "tensor"), None, None),
        P(),
        P(None, "seq"),
    )
    out_specs = (P(None, "tensor"), P())
    return jax.shard_map(body, mesh=mesh, in_specs=in_specs, out_specs=out_specs, check_vma=False)
```

profile of v0, /device:TPU:0, one launch (start us, length us, event | category | flops | bytes accessed | tf_op | source)
XLA Modules:
  0.0 235.1 jit_solution(18055280222267351378)
XLA Ops:
  8.1 4.3 %fusion.37 = bf16[1,528,16]{1,2,0:T(8,128)(2,1)S(1)} fusion(bf16[16,5120]{1,0:T(8,128)(2,1)} %param.11, bf16[5120,528]{0,1:T(8,128)(2,1)} %param.12), kind=kOutput, calls=%fused_computation.22 | convolution fusion | flops 86515968 | bytes 5587456 | tf_op jit(solution)/shard_map/dot_general | solution.py:113
  12.3 6.3 %all-gather = bf16[4,528,16]{1,2,0:T(8,128)(2,1)S(1)} all-gather(bf16[1,528,16]{1,2,0:T(8,128)(2,1)S(1)} %fusion.37), channel_id=1, replica_groups=mesh['seq'=8,'tensor'=4] {'tensor'}, dimensions={0}, use_global_device_ids=true | all-gather | bytes 84480 | tf_op jit(solution)/shard_map/all_gather | solution.py:116
  18.9 0.8 dynamic-slice
  19.7 0.5 fusion.62
  20.4 1.2 copy.83
  21.7 0.5 all-gather.6.cloned.1.call-update
  22.3 0.5 all-gather.4.cloned.1.call-update
  23.9 0.7 fusion.78
  24.6 71.6 %all-reduce.3.cloned.1.call-done = f32[16,32,192]{2,0,1:T(8,128)} async-done(((f32[16,32,192]{2,0,1:T(8,128)}), f32[16,32,192]{2,0,1:T(8,128)}) %all-reduce.3.cloned.1.call-update) | async-done | bytes 393232 | tf_op jit(solution)/shard_map/psum | solution.py:125
  96.2 1.2 multiply_subtract_fusion
  97.4 0.9 multiply_reduce_fusion.1
  98.2 4.2 %multiply_reduce_fusion = (f32[16,32]{0,1:T(8,128)}, bf16[16,32,512]{2,0,1:T(8,128)(2,1)S(1)}) fusion(f32[16,512]{1,0:T(8,128)S(1)} %get-tuple-element.8, f32[16,32,192]{2,0,1:T(8,128)} %all-reduce.3.cloned.1.call-done, bf16[512,4096]{1,0:T(8,128)(2,1)} %param.16), kind=kOutput, calls=%fused_computation.26 | convolution fusion | flops 68419072 | bytes 4884480 | tf_op jit(solution)/shard_map/bhn,khn->bhk/dot_general | solution.py:129
  102.4 0.9 convolution_convert_fusion
  103.3 1.6 slice.47
  105.0 2.7 %fusion.45 = f32[64,32,128]{2,1,0:T(8,128)} fusion(bf16[64,64,128]{2,1,0:T(8,128)(2,1)} %all-gather.6.cloned.1.call-done, bf16[64,32,64]{2,0,1:T(8,128)(2,1)S(1)} %slice.48), kind=kOutput, calls=%fused_computation.33 | convolution fusion | flops 33554432 | bytes 2359296 | tf_op jit(solution)/shard_map/khr,krp->khp/dot_general | solution.py:59
  107.7 6.7 %fusion.79 = (f32[64,32]{1,0:T(8,128)S(1)}, f32[64,32,128]{2,1,0:T(8,128)S(1)}) fusion(f32[64,32,128]{2,1,0:T(8,128)} %fusion.45, bf16[64,128,512]{2,1,0:T(8,128)(2,1)} %all-gather.4.cloned.1.call-done, bf16[64,32,512]{2,0,1:T(8,128)(2,1)} %slice.47, pred[64,128]{1,0:T(8,128)(4,1)S(1)} %add_compare_fusion), kind=kOutput, calls=%fused_computation.104 | convolution fusion | flops 269219840 | bytes 12599296 | tf_op jit(solution)/shard_map/khc,kpc->khp/dot_general | solution.py:53
  114.8 20.1 %pmax.7 = f32[16,32]{1,0:T(8,128)S(1)} all-reduce(f32[16,32]{1,0:T(8,128)S(1)} %broadcast_maximum_fusion), channel_id=1, replica_groups=mesh['seq'=8,'tensor'=4] {'seq'}, use_global_device_ids=true, to_apply=%region_8.9 | all-reduce | flops 512 | bytes 4096 | tf_op jit(solution)/shard_map/pmax | solution.py:151
  134.9 0.6 subtract_exponential_fusion.2
  135.6 1.4 copy.90
  137.0 1.4 copy.91
  138.4 4.3 %convolution_multiply_fusion = f32[64,32,512]{2,1,0:T(8,128)S(1)} fusion(bf16[64,128,512]{2,1,0:T(8,128)(2,1)} %all-gather.4.cloned.1.call-done, f32[64,32]{1,0:T(8,128)S(1)} %subtract_exponential_fusion, f32[64,32,128]{2,1,0:T(8,128)S(1)} %get-tuple-element.24, f32[64,32]{1,0:T(8,128)S(1)} %get-tuple-element.23, pred[64,128]{1,0:T(8,128)(4,1)S(1)} %add_compare_fusion), kind=kOutput, calls=%fused_computation.8 | convolution fusion | flops 270270464 | bytes 13656064 | tf_op jit(solution)/shard_map/khp,kpc->khc/dot_general | solution.py:70
  142.7 4.9 %fusion.19 = f32[16,32,512]{2,0,1:T(8,128)} fusion(f32[64,32,512]{2,1,0:T(8,128)S(1)} %convolution_multiply_fusion, f32[16,32]{0,1:T(8,128)S(1)} %copy-done.6, f32[16,32]{0,1:T(8,128)S(1)} %copy-done.5, s32[64]{0:T(128)S(1)} %copy-done.10), kind=kOutput, calls=%fused_computation.15 | convolution fusion | flops 201851904 | bytes 5247232 | tf_op jit(solution)/shard_map/kb,khc->bhc/dot_general | solution.py:83
  147.6 1.4 pad_maximum_fusion
  149.0 1.4 copy.93
  150.4 0.7 copy.92
  151.1 0.6 fusion.39
  151.7 0.8 fusion.38
  152.5 17.8 %psum.23 = f32[16,32]{1,0:T(8,128)S(1)} all-reduce(f32[16,32]{1,0:T(8,128)S(1)} %fusion.38), channel_id=1, replica_groups=mesh['seq'=8,'tensor'=4] {'seq'}, use_global_device_ids=true, to_apply=%region_14.15 | all-reduce | flops 512 | bytes 4096 | tf_op jit(solution)/shard_map/psum | solution.py:153
  170.3 0.7 multiply_add_fusion.1
  171.3 52.3 %all-reduce.5.cloned.1.call-done = f32[16,32,512]{2,0,1:T(8,128)} async-done(((f32[16,32,512]{2,0,1:T(8,128)}), f32[16,32,512]{2,0,1:T(8,128)}) %all-reduce.5.cloned.1.call-update) | async-done | bytes 1048592 | tf_op jit(solution)/shard_map/psum | solution.py:153
  223.5 3.5 %fusion.34 = bf16[32,2,8,128]{3,2,1,0:T(8,128)(2,1)S(1)} fusion(f32[16,32,512]{2,0,1:T(8,128)} %all-reduce.5.cloned.1.call-done, f32[16,32]{0,1:T(8,128)S(1)} %copy.96, f32[16,32]{0,1:T(8,128)S(1)} %copy.95, f32[16,32]{0,1:T(8,128)S(1)} %copy.94, f32[16,512]{1,0:T(8,128)S(1)} %get-tuple-element.8, bf16[512,4096]{1,0:T(8,128)(2,1)} %param.17), kind=kOutput, calls=%fused_computation.20 | convolution fusion | flops 68485120 | bytes 5412864 | tf_op jit(solution)/shard_map/bhk,khv->bhv/dot_general | solution.py:173
  227.0 0.7 copy.139
  (65 shorter events, 2.5 us)
Async XLA Ops:
  8.0 11.7 %copy-start = (bf16[192,6144]{1,0:T(8,128)(2,1)S(1)}, bf16[192,6144]{1,0:T(8,128)(2,1)}, u32[]{:S(2)}) copy-start(bf16[192,6144]{1,0:T(8,128)(2,1)} %param.15) | copy-start | bytes 7077892
  8.0 88.2 %all-reduce.3.cloned.1.call-start = ((), (), s32[]{:S(2)}) async-start(), calls=%async_computation | async-start | bytes 1048576 | tf_op jit(solution)/shard_map/psum | solution.py:125
  18.6 4.2 %copy-start.13 = (s32[16]{0:T(128)S(1)}, s32[16]{0:T(128)}, u32[]{:S(2)}) copy-start(s32[16]{0:T(128)} %param.20) | copy-start | bytes 196
  18.6 4.3 %copy-start.11 = (s32[16,4]{0,1:T(4,128)S(1)}, s32[16,4]{0,1:T(4,128)}, u32[]{:S(2)}) copy-start(s32[16,4]{0,1:T(4,128)} %param.21) | copy-start | bytes 772
  18.7 5.3 %copy-start.12 = (f32[512]{0:T(512)S(1)}, f32[512]{0:T(512)}, u32[]{:S(2)}) copy-start(f32[512]{0:T(512)} %param.14) | copy-start | bytes 6148
  21.6 83.4 %all-gather.6.cloned.1.call-start = ((), (), s32[]{:S(2)}) async-start(), calls=%async_computation.2 | async-start | bytes 1310720 | tf_op jit(solution)/shard_map/all_gather | solution.py:145
  22.2 85.5 %all-gather.4.cloned.1.call-start = ((), (), s32[]{:S(2)}) async-start(), calls=%async_computation.1 | async-start | bytes 10485760 | tf_op jit(solution)/shard_map/all_gather | solution.py:144
  22.8 200.7 %all-reduce.5.cloned.1.call-start = ((), (), s32[]{:S(2)}) async-start(), calls=%async_computation.3 | async-start | bytes 2097152 | tf_op jit(solution)/shard_map/psum | solution.py:153
  23.2 0.6 copy-start.7
  23.2 0.7 copy-start.8
  23.6 79.7 %copy-start.9 = (s32[64]{0:T(128)}, s32[64]{0:T(128)S(1)}, u32[]{:S(2)}) copy-start(s32[64]{0:T(128)S(1)} %get-tuple-element.3) | copy-start | bytes 772
  134.9 0.6 copy-start.1
  138.3 4.3 %copy-start.5 = (f32[16,32]{0,1:T(8,128)S(1)}, f32[16,32]{0,1:T(8,128)}, u32[]{:S(2)}) copy-start(f32[16,32]{0,1:T(8,128)} %copy.90) | copy-start | bytes 6148
  138.3 4.3 %copy-start.6 = (f32[16,32]{0,1:T(8,128)S(1)}, f32[16,32]{0,1:T(8,128)}, u32[]{:S(2)}) copy-start(f32[16,32]{0,1:T(8,128)} %copy.91) | copy-start | bytes 6148
  138.3 4.3 %copy-start.10 = (s32[64]{0:T(128)S(1)}, s32[64]{0:T(128)}, u32[]{:S(2)}) copy-start(s32[64]{0:T(128)} %copy-done.9) | copy-start | bytes 772
  142.6 7.8 %copy-start.4 = (f32[16,32]{0,1:T(8,128)S(1)}, f32[16,32]{0,1:T(8,128)}, u32[]{:S(2)}) copy-start(f32[16,32]{0,1:T(8,128)} %get-tuple-element.25) | copy-start | bytes 6148
  142.7 9.1 %copy-start.3 = (f32[16,32]{1,0:T(8,128)S(1)}, f32[16,32]{1,0:T(8,128)}, u32[]{:S(2)}) copy-start(f32[16,32]{1,0:T(8,128)} %get-tuple-element.18) | copy-start | bytes 6148
  142.7 27.6 %copy-start.2 = (f32[16,32]{1,0:T(8,128)S(1)}, f32[16,32]{1,0:T(8,128)}, u32[]{:S(2)}) copy-start(f32[16,32]{1,0:T(8,128)} %copy-done.1) | copy-start | bytes 6148
Sparse Core Ops, SparseCore 0:
  21.8 74.3 all-reduce.2
  147.7 75.7 all-reduce.4
Sparse Core Ops, SparseCore 1:
  23.7 18.3 all-gather.5
  43.4 58.1 all-gather.3
where the time goes:
time: 236 us; the launch traced here: 235 us
  waiting for transfers between devices  125 us (53%)
  blocking collectives  44.2 us (19%)
  matrix products  32.6 us (14%)
  between operations  15.8 us (7%)
  local copies, waits for them, and re-layouts  10.2 us (4%)
  other arithmetic  7.24 us (3%)
    psum x1, waiting for transfers between devices, body(): query_full = lax.psum(partial_query, 'seq').reshape(B, local_heads, QH)  71.6 us
    psum x1, waiting for transfers between devices, body(): lax.psum((total_part * factor, mixed_part * factor[:, :, None]), 'seq')  52.3 us
    pmax x1, blocking collectives, body(): grand_top = lax.pmax(top_part, 'seq')  20.1 us
    psum x1, blocking collectives, body(): lax.psum((total_part * factor, mixed_part * factor[:, :, None]), 'seq')  17.8 us
    dot_general x1, matrix products, attend_slots(): jnp.einsum('khc,kpc->khp', picked[:, :, :latent_width], latent_blocks, pr...  6.66 us
    all_gather x1, blocking collectives, body(): lax.all_gather(part_cols, 'tensor', axis=1, tiled=True).astype(jnp.float32)  6.27 us
    dot_general x1, matrix products, attend_slots(): jnp.einsum('kb,khc->bhc', hot_wide, slot_mixed * factor[:, :, None], prec...  4.91 us
  transfers between devices with their start and end apart: 4, of which 2 were waited for; matrix products, arithmetic and copies ran while one was open for 8% of the time, Pallas kernels for 0%

commit v1 on v0

--- a/solution.py
+++ b/solution.py
@@ -1,6 +1,10 @@
+import functools
+
 import jax
 import jax.numpy as jnp
 from jax import lax
+from jax.experimental import pallas as pl
+from jax.experimental.pallas import tpu as pltpu
 from jax.sharding import PartitionSpec as P
 
 QR = 1536
@@ -94,7 +98,7 @@
     return (top_both, total_two * scale_two, mixed_two * scale_two[:, :, None])
 
 
-def body(
+def plain_body(
     hidden_in,
     united_down,
     q_gain,
@@ -175,6 +179,603 @@
     return (attn_out, new_entry)
 
 
+MESH_ID = pl.DeviceIdType.MESH
+LANES = 128
+UNITED_CHUNKS = 5
+GROUP = 4
+
+
+def split_three(value):
+    high = value.astype(jnp.bfloat16)
+    rest = value - high.astype(jnp.float32)
+    middle = rest.astype(jnp.bfloat16)
+    low = (rest - middle.astype(jnp.float32)).astype(jnp.bfloat16)
+    return high, middle, low
+
+
+def rotate_wide(wide, cos_wide, sin_wide, lane_at, half):
+    partner = jnp.where(
+        lane_at < half, pltpu.roll(wide, LANES - half, 1), pltpu.roll(wide, half, 1)
+    )
+    return wide * cos_wide + partner * sin_wide
+
+
+def step_kernel(
+    n_seq,
+    n_tensor,
+    dims,
+    idx_ref,
+    len_ref,
+    hidden_ref,
+    cos_ref,
+    sin_ref,
+    q_gain_ref,
+    kv_gain_ref,
+    ud_hbm,
+    qu_hbm,
+    ku_hbm,
+    vu_hbm,
+    lat_hbm,
+    rope_hbm,
+    out_ref,
+    ne_ref,
+    ud_vm,
+    qu_vm,
+    ku_vm,
+    vu_vm,
+    lat_vm,
+    rope_vm,
+    uni_vm,
+    uw_vm,
+    ql_vm,
+    nep_vm,
+    qs_vm,
+    qr_vm,
+    pack_vm,
+    qall_vm,
+    mix_vm,
+    top_vm,
+    tot_vm,
+    mixall_vm,
+    part_vm,
+    got_vm,
+    out_vm,
+    ud_sem,
+    w_sem,
+    loc_sem,
+    u_send,
+    u_recv,
+    y_send,
+    y_recv,
+    c_send,
+    c_recv,
+    d_send,
+    d_recv,
+    q_send,
+    q_recv,
+    p_send,
+    p_recv,
+    m_send,
+    m_recv,
+    o_send,
+    o_recv,
+):
+    heads = dims["heads"]
+    own_heads = dims["own_heads"]
+    batch = dims["batch"]
+    span_blocks = dims["span_blocks"]
+    blocks = dims["blocks"]
+    united_cols = dims["united_cols"]
+    rope_width = dims["rope_width"]
+    rows = dims["rows"]
+    rank = LATENT_RANK
+    pack_width = rank + LANES
+    own_rows = own_heads * batch
+    all_rows = heads * batch
+    groups = blocks // GROUP
+    s = lax.axis_index("seq")
+    t = lax.axis_index("tensor")
+    core_mate = t + 1 - 2 * (t % 2)
+    far_mate = (t + 2) % n_tensor
+    diagonal = (core_mate + 2) % n_tensor
+
+    def at_seq(i):
+        return {"seq": (s + i) % n_seq}
+
+    depth = hidden_ref.shape[1] // UNITED_CHUNKS
+    ud_copies = [
+        pltpu.make_async_copy(
+            ud_hbm.at[pl.ds(i * depth, depth)], ud_vm.at[pl.ds(i * depth, depth)], ud_sem.at[i]
+        )
+        for i in range(UNITED_CHUNKS)
+    ]
+    for copy in ud_copies:
+        copy.start()
+    head_cols = pl.ds(pl.multiple_of(s * (own_heads * NOPE), LANES), own_heads * NOPE)
+    qu_copy = pltpu.make_async_copy(qu_hbm, qu_vm, w_sem.at[0])
+    ku_copy = pltpu.make_async_copy(ku_hbm.at[:, head_cols], ku_vm, w_sem.at[1])
+    vu_copy = pltpu.make_async_copy(vu_hbm.at[:, head_cols], vu_vm, w_sem.at[2])
+    lat_copy = pltpu.make_async_copy(lat_hbm, lat_vm.at[t], loc_sem.at[0])
+    rope_copy = pltpu.make_async_copy(rope_hbm, rope_vm.at[t], loc_sem.at[1])
+    for copy in (qu_copy, ku_copy, vu_copy, lat_copy, rope_copy):
+        copy.start()
+
+    barrier = pltpu.get_barrier_semaphore()
+    for i in range(1, n_seq):
+        pl.semaphore_signal(barrier, inc=1, device_id=at_seq(i), device_id_type=MESH_ID)
+    for i in range(1, n_tensor):
+        pl.semaphore_signal(
+            barrier, inc=1, device_id={"tensor": (t + i) % n_tensor}, device_id_type=MESH_ID
+        )
+    pl.semaphore_wait(barrier, n_seq - 1 + n_tensor - 1)
+
+    def block_copies(src_lat, src_rope, owner, c, send, recv, target):
+        at = pl.ds(c * GROUP, GROUP)
+        return (
+            pltpu.make_async_remote_copy(
+                src_ref=src_lat.at[at],
+                dst_ref=lat_vm.at[owner, at],
+                send_sem=send.at[c, 0],
+                recv_sem=recv.at[c, 0],
+                device_id={"tensor": target},
+                device_id_type=MESH_ID,
+            ),
+            pltpu.make_async_remote_copy(
+                src_ref=src_rope.at[at],
+                dst_ref=rope_vm.at[owner, at],
+                send_sem=send.at[c, 1],
+                recv_sem=recv.at[c, 1],
+                device_id={"tensor": target},
+                device_id_type=MESH_ID,
+            ),
+        )
+
+    def y_copies(c):
+        return block_copies(lat_hbm, rope_hbm, t, c, y_send, y_recv, far_mate)
+
+    def c_copies(c):
+        return block_copies(lat_hbm, rope_hbm, t, c, c_send, c_recv, core_mate)
+
+    def d_copies(c):
+        return block_copies(
+            lat_vm.at[far_mate], rope_vm.at[far_mate], far_mate, c, d_send, d_recv, core_mate
+        )
+
+    total = jnp.zeros((batch, united_cols), jnp.float32)
+    for i, copy in enumerate(ud_copies):
+        copy.wait()
+        total = total + jnp.dot(
+            hidden_ref[:, i * depth : (i + 1) * depth],
+            ud_vm[i * depth : (i + 1) * depth, :],
+            preferred_element_type=jnp.float32,
+        )
+    uni_vm[t] = jnp.zeros(uni_vm.shape[1:], jnp.bfloat16)
+    uni_vm[t, :, :united_cols] = total.astype(jnp.bfloat16)
+
+    def u_copy(i):
+        return pltpu.make_async_remote_copy(
+            src_ref=uni_vm.at[t],
+            dst_ref=uni_vm.at[t],
+            send_sem=u_send.at[i],
+            recv_sem=u_recv.at[i],
+            device_id={"tensor": (t + i) % n_tensor},
+            device_id_type=MESH_ID,
+        )
+
+    u_copies = [u_copy(i) for i in range(1, n_tensor)]
+    for copy in u_copies:
+        copy.start()
+    for c in range(groups):
+        for copy in y_copies(c):
+            copy.start()
+    for c in range(groups):
+        for copy in c_copies(c):
+            copy.start()
+    for copy in u_copies:
+        copy.wait()
+    uw_vm[...] = jnp.zeros(uw_vm.shape, jnp.float32)
+    wide_cols = uni_vm.shape[2]
+    for i in range(n_tensor):
+        base = united_cols * i // LANES * LANES
+        shift = united_cols * i - base
+        piece = uni_vm[i].astype(jnp.float32)
+        if shift:
+            piece = pltpu.roll(piece, shift, 1)
+        uw_vm[:, base : base + wide_cols] = uw_vm[:, base : base + wide_cols] + piece
+
+    lane_at = lax.broadcasted_iota(jnp.int32, (batch, LANES), 1)
+    half = rope_width // 2
+    cos_wide = cos_ref[...]
+    sin_wide = sin_ref[...]
+    latent_part = uw_vm[:, :QR]
+    ql_vm[...] = rms_scale(latent_part, q_gain_ref[...]).astype(jnp.bfloat16).astype(jnp.float32)
+    new_latent = rms_scale(uw_vm[:, QR : QR + rank], kv_gain_ref[...]).astype(jnp.bfloat16)
+    new_rope = rotate_wide(
+        uw_vm[:, QR + rank : QR + rank + LANES], cos_wide, sin_wide, lane_at, half
+    ).astype(jnp.bfloat16)
+    ne_ref[:, :rank] = new_latent
+    ne_ref[:, rank:] = new_rope[:, :rope_width]
+    nep_vm[:, :rank] = new_latent.astype(jnp.float32)
+    nep_vm[:, rank:] = new_rope.astype(jnp.float32)
+
+    row_base = pl.multiple_of(s * rows // LANES * LANES, LANES)
+    row_window = ql_vm[:, pl.ds(row_base, 2 * LANES)]
+    row_window = jnp.where(
+        (s * rows) % LANES == 0, row_window, pltpu.roll(row_window, 2 * LANES - LANES // 2, 1)
+    )
+    own_query = row_window[:, :rows].astype(jnp.bfloat16)
+    qu_copy.wait()
+    chunk_cols = own_heads * QH
+
+    def q_copy(i):
+        return pltpu.make_async_remote_copy(
+            src_ref=qs_vm.at[i],
+            dst_ref=qr_vm.at[i],
+            send_sem=q_send.at[i],
+            recv_sem=q_recv.at[i],
+            device_id=at_seq(i),
+            device_id_type=MESH_ID,
+        )
+
+    for i in list(range(1, n_seq)) + [0]:
+        cols = pl.ds(pl.multiple_of((s + i) % n_seq * chunk_cols, LANES), chunk_cols)
+        qs_vm[i] = jnp.dot(own_query, qu_vm[:, cols], preferred_element_type=jnp.float32)
+        if i:
+            q_copy(i).start()
+    query = qs_vm[0]
+    for i in range(1, n_seq):
+        q_copy(i).wait()
+        query = query + qr_vm[i]
+
+    score_scale = QH ** (-0.5)
+    ku_copy.wait()
+    pair = 2 * QH
+    for h in range(own_heads):
+        both = query[:, h // 2 * pair : (h // 2 + 1) * pair]
+        start = 0
+        if h % 2:
+            both = pltpu.roll(both, pair - LANES // 2, 1)
+            start = LANES
+        nope = both[:, start : start + NOPE].astype(jnp.bfloat16)
+        if h % 2:
+            rope = both[:, 2 * LANES : 3 * LANES]
+        else:
+            rope = both[:, LANES : 2 * LANES]
+        absorbed = lax.dot_general(
+            nope,
+            ku_vm[:, h * NOPE : (h + 1) * NOPE],
+            (((1,), (1,)), ((), ())),
+            preferred_element_type=jnp.float32,
+        )
+        at = pl.ds(h * batch, batch)
+        pack_vm[0, at, :rank] = (absorbed * score_scale).astype(jnp.bfloat16)
+        pack_vm[0, at, rank:] = (
+            rotate_wide(rope, cos_wide, sin_wide, lane_at, half) * score_scale
+        ).astype(jnp.bfloat16)
+
+    def p_copy(i):
+        return pltpu.make_async_remote_copy(
+            src_ref=pack_vm.at[0],
+            dst_ref=pack_vm.at[i],
+            send_sem=p_send.at[i],
+            recv_sem=p_recv.at[i],
+            device_id=at_seq(i),
+            device_id_type=MESH_ID,
+        )
+
+    for i in range(1, n_seq):
+        p_copy(i).start()
+    for i in range(1, n_seq):
+        p_copy(i).wait()
+    for b0 in range(0, batch, 4):
+        part_rows = 4 * heads
+        want = lax.broadcasted_iota(jnp.int32, (part_rows, all_rows), 0)
+        have = lax.broadcasted_iota(jnp.int32, (part_rows, all_rows), 1)
+        want_b = b0 + want // heads
+        want_h = want % heads
+        slot = (s + n_seq - want_h // own_heads) % n_seq
+        source = slot * own_rows + want_h % own_heads * batch + want_b
+        hot = jnp.where(have == source, 1.0, 0.0).astype(jnp.bfloat16)
+        ordered = jnp.dot(
+            hot,
+            pack_vm[...].reshape(all_rows, pack_width),
+            preferred_element_type=jnp.float32,
+        ).astype(jnp.bfloat16)
+        qall_vm[b0 : b0 + 4] = ordered.reshape(4, heads, pack_width)
+
+    position = lax.broadcasted_iota(jnp.int32, (heads, BLOCK_POSITIONS), 1)
+
+    def attend_one(owner, k):
+        slot = owner * blocks + k
+        flat = idx_ref[slot]
+        seq_of = flat // span_blocks
+        base = (s * span_blocks + flat % span_blocks) * BLOCK_POSITIONS
+        limit = len_ref[seq_of] - base
+        q = qall_vm[seq_of]
+        latent = lat_vm[owner, k]
+        scores = lax.dot_general(
+            q[:, :rank], latent, (((1,), (1,)), ((), ())), preferred_element_type=jnp.float32
+        )
+        scores = scores + jnp.dot(
+            q[:, rank : rank + rope_width], rope_vm[owner, k], preferred_element_type=jnp.float32
+        )
+        valid = position < limit
+        scores = jnp.where(valid, scores, FLOOR_SCORE)
+        top = jnp.max(scores, axis=1, keepdims=True)
+        weights = jnp.where(valid, jnp.exp(scores - top), 0.0)
+        amount = jnp.sum(weights, axis=1, keepdims=True)
+        mixed = jnp.dot(weights.astype(jnp.bfloat16), latent, preferred_element_type=jnp.float32)
+        mix_vm[slot] = mixed
+        top_vm[slot] = jnp.broadcast_to(top, (heads, LANES))
+        tot_vm[slot] = jnp.broadcast_to(amount, (heads, LANES))
+
+    def attend_group(owner, c):
+        for k in range(GROUP):
+            attend_one(owner, c * GROUP + k)
+
+    lat_copy.wait()
+    rope_copy.wait()
+
+    def own_step(c, carry):
+        attend_group(t, c)
+        return carry
+
+    lax.fori_loop(0, groups, own_step, 0)
+
+    def mate_step(c, carry):
+        for copy in c_copies(c):
+            copy.wait()
+        attend_group(core_mate, c)
+        return carry
+
+    lax.fori_loop(0, groups, mate_step, 0)
+
+    def far_step(c, carry):
+        for copy in y_copies(c):
+            copy.wait()
+        for copy in d_copies(c):
+            copy.start()
+        attend_group(far_mate, c)
+        for copy in d_copies(c):
+            copy.wait()
+        attend_group(diagonal, c)
+        return carry
+
+    lax.fori_loop(0, groups, far_step, 0)
+
+    lane_wide = lax.broadcasted_iota(jnp.int32, (heads, LANES), 1)
+
+    def merge_step(b, carry):
+        slots = [idx_ref[n_tensor * blocks + b * span_blocks + j] for j in range(span_blocks)]
+        tops = [top_vm[slot] for slot in slots]
+        top = functools.reduce(jnp.maximum, tops)
+        total = jnp.zeros((heads, LANES), jnp.float32)
+        mixed = jnp.zeros((heads, rank), jnp.float32)
+        for slot, one in zip(slots, tops):
+            factor = jnp.exp(one - top)
+            total = total + tot_vm[slot] * factor
+            mixed = mixed + mix_vm[slot] * factor[:, :1]
+        stats = jnp.zeros((heads, LANES), jnp.float32)
+        for lane, piece in enumerate(split_three(top) + split_three(total)):
+            stats = jnp.where(lane_wide == lane, piece.astype(jnp.float32), stats)
+        at = pl.ds(pl.multiple_of(b * heads, heads), heads)
+        mixall_vm[at, :rank] = mixed.astype(jnp.bfloat16)
+        mixall_vm[at, rank:] = stats.astype(jnp.bfloat16)
+        return carry
+
+    lax.fori_loop(0, batch, merge_step, 0)
+
+    def m_copy(i):
+        return pltpu.make_async_remote_copy(
+            src_ref=part_vm.at[i],
+            dst_ref=got_vm.at[i],
+            send_sem=m_send.at[i],
+            recv_sem=m_recv.at[i],
+            device_id=at_seq(i),
+            device_id_type=MESH_ID,
+        )
+
+    want = lax.broadcasted_iota(jnp.int32, (own_rows, all_rows), 0)
+    have = lax.broadcasted_iota(jnp.int32, (own_rows, all_rows), 1)
+    local_source = want % batch * heads + want // batch
+    for i in list(range(1, n_seq)) + [0]:
+        peer = (s + i) % n_seq
+        hot = jnp.where(have == local_source + peer * own_heads, 1.0, 0.0).astype(jnp.bfloat16)
+        chosen = jnp.dot(hot, mixall_vm[...], preferred_element_type=jnp.float32).astype(
+            jnp.bfloat16
+        )
+        if i:
+            part_vm[i] = chosen
+            m_copy(i).start()
+        else:
+            got_vm[0] = chosen
+
+    pack = pack_vm[0].astype(jnp.float32)
+    entry = jnp.concatenate([nep_vm[...]] * own_heads, axis=0)
+    own_score = jnp.sum(pack * entry, axis=1, keepdims=True)
+    for i in range(1, n_seq):
+        m_copy(i).wait()
+    tops = []
+    totals = []
+    for i in range(n_seq):
+        stats = got_vm[i, :, rank:].astype(jnp.float32)
+        tops.append(stats[:, 0:1] + stats[:, 1:2] + stats[:, 2:3])
+        totals.append(stats[:, 3:4] + stats[:, 4:5] + stats[:, 5:6])
+    final_top = functools.reduce(jnp.maximum, tops, own_score)
+    own_weight = jnp.exp(own_score - final_top)
+    total = own_weight
+    mixture = own_weight.astype(jnp.bfloat16).astype(jnp.float32) * entry[:, :rank]
+    for i in range(n_seq):
+        factor = jnp.exp(tops[i] - final_top)
+        total = total + totals[i] * factor
+        mixture = mixture + got_vm[i, :, :rank].astype(jnp.float32) * factor
+    attended = (mixture / total).astype(jnp.bfloat16)
+    vu_copy.wait()
+    for h in range(own_heads):
+        out_vm[0, :, h * VD : (h + 1) * VD] = jnp.dot(
+            attended[h * batch : (h + 1) * batch],
+            vu_vm[:, h * VD : (h + 1) * VD],
+            preferred_element_type=jnp.float32,
+        ).astype(jnp.bfloat16)
+
+    def o_copy(i):
+        return pltpu.make_async_remote_copy(
+            src_ref=out_vm.at[0],
+            dst_ref=out_vm.at[i],
+            send_sem=o_send.at[i],
+            recv_sem=o_recv.at[i],
+            device_id=at_seq(i),
+            device_id_type=MESH_ID,
+        )
+
+    for i in range(1, n_seq):
+        o_copy(i).start()
+    for i in range(n_seq):
+        if i:
+            o_copy(i).wait()
+        cols = pl.ds(
+            pl.multiple_of((s + n_seq - i) % n_seq * (own_heads * VD), LANES), own_heads * VD
+        )
+        out_ref[:, cols] = out_vm[i]
+
+
+def kernel_body(
+    n_seq,
+    n_tensor,
+    hidden_in,
+    united_down,
+    q_gain,
+    kv_gain,
+    q_up,
+    key_up,
+    value_up,
+    latent_block_store,
+    rope_pool,
+    lengths,
+    block_table,
+):
+    batch, width = hidden_in.shape
+    heads = key_up.shape[1] // NOPE
+    own_heads = heads // n_seq
+    span_blocks = block_table.shape[1]
+    blocks = latent_block_store.shape[0]
+    rope_width = rope_pool.shape[1]
+    united_cols = united_down.shape[1]
+    seq_index = lax.axis_index("seq")
+    local_table = block_table.reshape(-1) - seq_index * (batch * span_blocks)
+    flat_index = jnp.arange(local_table.shape[0], dtype=jnp.int32)
+    slot_at = jnp.arange(n_tensor * blocks, dtype=jnp.int32)
+    owner = jnp.sum(
+        jnp.where(local_table[None, :] == slot_at[:, None], flat_index[None, :], 0), axis=1
+    )
+    places = jnp.concatenate([owner, local_table])
+    half = rope_width // 2
+    lane = jnp.arange(LANES, dtype=jnp.int32)
+    freq = 10000.0 ** (-2.0 * (lane % half).astype(jnp.float32) / rope_width)
+    angles = lengths.astype(jnp.float32)[:, None] * freq[None, :]
+    inside = (lane < rope_width)[None, :]
+    cos_wide = jnp.where(inside, jnp.cos(angles), 0.0)
+    sine = jnp.sin(angles)
+    sin_wide = jnp.where(inside, jnp.where((lane < half)[None, :], -sine, sine), 0.0)
+    dims = dict(
+        heads=heads,
+        own_heads=own_heads,
+        batch=batch,
+        span_blocks=span_blocks,
+        blocks=blocks,
+        united_cols=united_cols,
+        rope_width=rope_width,
+        rows=q_up.shape[0],
+    )
+    wide_cols = -(-united_cols // LANES) * LANES
+    united_all = -(-united_cols * n_tensor // LANES) * LANES + 4 * LANES
+    pack_width = LATENT_RANK + LANES
+    own_rows = own_heads * batch
+    all_rows = heads * batch
+    groups = blocks // GROUP
+    slots = n_tensor * blocks
+    vmem = pl.BlockSpec(memory_space=pltpu.VMEM)
+    smem = pl.BlockSpec(memory_space=pltpu.SMEM)
+    anywhere = pl.BlockSpec(memory_space=pl.ANY)
+    dma = pltpu.SemaphoreType.DMA
+    bf16, f32 = jnp.bfloat16, jnp.float32
+    out, new_entry = pl.pallas_call(
+        functools.partial(step_kernel, n_seq, n_tensor, dims),
+        out_shape=(
+            jax.ShapeDtypeStruct((batch, heads * VD), bf16),
+            jax.ShapeDtypeStruct((batch, LATENT_RANK + rope_width), bf16),
+        ),
+        in_specs=[smem, smem] + [vmem] * 5 + [anywhere] * 6,
+        out_specs=(vmem, vmem),
+        scratch_shapes=[
+            pltpu.VMEM(united_down.shape, bf16),
+            pltpu.VMEM(q_up.shape, bf16),
+            pltpu.VMEM((LATENT_RANK, own_heads * NOPE), bf16),
+            pltpu.VMEM((LATENT_RANK, own_heads * VD), bf16),
+            pltpu.VMEM((n_tensor,) + latent_block_store.shape, bf16),
+            pltpu.VMEM((n_tensor,) + rope_pool.shape, bf16),
+            pltpu.VMEM((n_tensor, batch, wide_cols), bf16),
+            pltpu.VMEM((batch, united_all), f32),
+            pltpu.VMEM((batch, QR), f32),
+            pltpu.VMEM((batch, pack_width), f32),
+            pltpu.VMEM((n_seq, batch, own_heads * QH), f32),
+            pltpu.VMEM((n_seq, batch, own_heads * QH), f32),
+            pltpu.VMEM((n_seq, own_rows, pack_width), bf16),
+            pltpu.VMEM((batch, heads, pack_width), bf16),
+            pltpu.VMEM((slots, heads, LATENT_RANK), f32),
+            pltpu.VMEM((slots, heads, LANES), f32),
+            pltpu.VMEM((slots, heads, LANES), f32),
+            pltpu.VMEM((all_rows, pack_width), bf16),
+            pltpu.VMEM((n_seq, own_rows, pack_width), bf16),
+            pltpu.VMEM((n_seq, own_rows, pack_width), bf16),
+            pltpu.VMEM((n_seq, batch, own_heads * VD), bf16),
+            dma((UNITED_CHUNKS,)),
+            dma((3,)),
+            dma((2,)),
+            dma((n_tensor,)),
+            dma((n_tensor,)),
+            dma((groups, 2)),
+            dma((groups, 2)),
+            dma((groups, 2)),
+            dma((groups, 2)),
+            dma((groups, 2)),
+            dma((groups, 2)),
+        ]
+        + [dma((n_seq,))] * 8,
+        compiler_params=pltpu.CompilerParams(
+            collective_id=0, has_side_effects=True, vmem_limit_bytes=60 * 1024 * 1024
+        ),
+    )(
+        places,
+        lengths,
+        hidden_in,
+        cos_wide,
+        sin_wide,
+        q_gain[None, :],
+        kv_gain[None, :],
+        united_down,
+        q_up,
+        key_up,
+        value_up,
+        latent_block_store,
+        rope_pool,
+    )
+    return (out, new_entry)
+
+
+def body_for(n_seq, n_tensor):
+    def body(*args):
+        q_up, key_up, latents = args[4], args[5], args[7]
+        heads = key_up.shape[1] // NOPE
+        fits = n_tensor == 4 and heads % (2 * n_seq) == 0 and latents.shape[0] % GROUP == 0
+        fits = fits and q_up.shape[0] % (LANES // 2) == 0 and q_up.shape[0] <= LANES + LANES // 2
+        if fits:
+            return kernel_body(n_seq, n_tensor, *args)
+        return plain_body(*args)
+
+    return body
+
+
 def solution(mesh):
     in_specs = (
         P(),
@@ -190,4 +791,5 @@
         P(None, "seq"),
     )
     out_specs = (P(None, "tensor"), P())
-    return jax.shard_map(body, mesh=mesh, in_specs=in_specs, out_specs=out_specs, check_vma=False)
+    return jax.shard_map(
+        body_for(mesh.shape["seq"], mesh.shape["tensor"]), mesh=mesh, in_specs=in_specs, out_specs=out_specs, check_vma=False)

time: 236 us -> 108 us (0.46)
  waiting for transfers between devices: 125 us -> 0 us
  Pallas kernels: 0 us -> 91.7 us
  blocking collectives: 44.2 us -> 0 us
  matrix products: 32.6 us -> 0 us
  between operations: 15.8 us -> 0.65 us
  other arithmetic: 7.24 us -> 2.8 us
  local copies, waits for them, and re-layouts: 10.2 us -> 12.8 us
    psum x2 -> x0, waiting for transfers between devices: 124 us -> none  [the longest x1 71.6 us: body(): query_full = lax.psum(partial_query, 'seq').reshape(B, local_heads, QH)]
    pallas_call x0 -> x1, Pallas kernels: none -> 91.7 us  [kernel_body(): pl.pallas_call(functools.partial(step_kernel, n_seq, n_tensor, dims), out...]
    dot_general x10 -> x0, matrix products: 32.6 us -> none  [the longest x1 6.66 us: attend_slots(): jnp.einsum('khc,kpc->khp', picked[:, :, :latent_width], latent_blocks, pr...]
    pmax x1 -> x0, blocking collectives: 20.1 us -> none  [body(): grand_top = lax.pmax(top_part, 'seq')]
    psum x1 -> x0, blocking collectives: 17.8 us -> none  [body(): lax.psum((total_part * factor, mixed_part * factor[:, :, None]), 'seq')]
    unnamed x29 -> x3, local copies, waits for them, and re-layouts: 0.23 us -> 11.3 us
    all_gather x1 -> x0, blocking collectives: 6.27 us -> none  [body(): lax.all_gather(part_cols, 'tensor', axis=1, tiled=True).astype(jnp.float32)]
    exp x3 -> x0, local copies, waits for them, and re-layouts: 2.82 us -> none  [the longest x1 1.38 us: body(): factor = jnp.exp(top_part - grand_top)]
  transfers between devices with their start and end apart: 4 -> 0, of which waited for: 2 -> 0; matrix products, arithmetic and copies ran while one was open for 8% -> 0% of each run, Pallas kernels for 0% -> 0%
where the time goes in v1:
time: 108 us
  Pallas kernels  91.7 us (85%)
  local copies, waits for them, and re-layouts  12.8 us (12%)
  other arithmetic  2.8 us (3%)
    pallas_call x1, Pallas kernels, kernel_body(): pl.pallas_call(functools.partial(step_kernel, n_seq, n_tensor, dims), out...  91.7 us
    unnamed x3, local copies, waits for them, and re-layouts  11.3 us

profile of v1, /device:TPU:0, one launch (start us, length us, event | category | flops | bytes accessed | tf_op | source)
XLA Modules:
  0.0 107.9 jit_solution(11434067401307824592)
XLA Ops:
  0.6 0.7 convert_element_type.10
  1.3 0.7 broadcast_subtract_fusion
  2.0 0.1 copy.17
  2.1 0.1 sub.15
  2.2 0.1 select_reduce_fusion
  2.3 0.6 pad_add_fusion.idx_ref
  2.9 1.3 %broadcast_in_dim.56.q_gain_ref = f32[1,1536]{1,0:T(1,128)} reshape(f32[1536]{0:T(1024)} %param.13) | data formatting | bytes 12288 | tf_op jit(solution)/shard_map/broadcast_in_dim | solution.py:754
  4.2 0.7 fusion.1
  4.9 8.4 %copy.18.ud_hbm = bf16[5120,528]{1,0:T(8,128)(2,1)} copy(bf16[5120,528]{0,1:T(8,128)(2,1)} %param.12) | data formatting | bytes 10813440 | tf_op args[1]
  13.3 91.7 %shard_map.122 = (bf16[16,4096]{1,0:T(8,128)(2,1)}, bf16[16,576]{1,0:T(8,128)(2,1)}) custom-call(s32[128]{0:T(128)} %pad_add_fusion.idx_ref, s32[16]{0:T(128)} %len_ref.1, bf16[16,5120]{1,0:T(8,128)(2,1)} %hidden_ref.1, f32[16,128]{1,0:T(8,128)} %get-tuple-element.3.cos_ref, f32[16,128]{1,0:T(8,128)} %get-tuple-element.2.sin_ref, ...), custom_call_target="tpu_custom_call" | custom-call | tf_op jit(solution)/shard_map/pallas_call | solution.py:702
  105.0 1.6 %copy.21 = bf16[16,4096]{1,0:T(8,128)(2,1)} copy(bf16[16,4096]{1,0:T(8,128)(2,1)} %get-tuple-element.8) | data formatting | bytes 262144
  106.6 1.3 %copy.22 = bf16[16,576]{1,0:T(8,128)(2,1)} copy(bf16[16,576]{1,0:T(8,128)(2,1)} %get-tuple-element.9) | data formatting | bytes 36864
  (2 shorter events, 0.0 us)

commit v2 on v1

--- a/solution.py
+++ b/solution.py
@@ -1,4 +1,5 @@
 import functools
+import math
 
 import jax
 import jax.numpy as jnp
@@ -207,8 +208,6 @@
     idx_ref,
     len_ref,
     hidden_ref,
-    cos_ref,
-    sin_ref,
     q_gain_ref,
     kv_gain_ref,
     ud_hbm,
@@ -285,7 +284,9 @@
     depth = hidden_ref.shape[1] // UNITED_CHUNKS
     ud_copies = [
         pltpu.make_async_copy(
-            ud_hbm.at[pl.ds(i * depth, depth)], ud_vm.at[pl.ds(i * depth, depth)], ud_sem.at[i]
+            ud_hbm.at[:, pl.ds(i * depth, depth)],
+            ud_vm.at[:, pl.ds(i * depth, depth)],
+            ud_sem.at[i],
         )
         for i in range(UNITED_CHUNKS)
     ]
@@ -344,9 +345,10 @@
     total = jnp.zeros((batch, united_cols), jnp.float32)
     for i, copy in enumerate(ud_copies):
         copy.wait()
-        total = total + jnp.dot(
+        total = total + lax.dot_general(
             hidden_ref[:, i * depth : (i + 1) * depth],
-            ud_vm[i * depth : (i + 1) * depth, :],
+            ud_vm[:, i * depth : (i + 1) * depth],
+            (((1,), (1,)), ((), ())),
             preferred_element_type=jnp.float32,
         )
     uni_vm[t] = jnp.zeros(uni_vm.shape[1:], jnp.bfloat16)
@@ -385,11 +387,18 @@
 
     lane_at = lax.broadcasted_iota(jnp.int32, (batch, LANES), 1)
     half = rope_width // 2
-    cos_wide = cos_ref[...]
-    sin_wide = sin_ref[...]
+    row_at = lax.broadcasted_iota(jnp.int32, (batch, LANES), 0)
+    positions = jnp.zeros((batch, LANES), jnp.float32)
+    for b in range(batch):
+        positions = jnp.where(row_at == b, len_ref[b].astype(jnp.float32), positions)
+    freq = jnp.exp((lane_at % half).astype(jnp.float32) * (-2.0 * math.log(10000.0) / rope_width))
+    angles = positions * freq
+    cos_wide = jnp.where(lane_at < rope_width, jnp.cos(angles), 0.0)
+    sine = jnp.sin(angles)
+    sin_wide = jnp.where(lane_at < half, -sine, jnp.where(lane_at < rope_width, sine, 0.0))
     latent_part = uw_vm[:, :QR]
-    ql_vm[...] = rms_scale(latent_part, q_gain_ref[...]).astype(jnp.bfloat16).astype(jnp.float32)
-    new_latent = rms_scale(uw_vm[:, QR : QR + rank], kv_gain_ref[...]).astype(jnp.bfloat16)
+    ql_vm[...] = rms_scale(latent_part, q_gain_ref[...].reshape(1, QR)).astype(jnp.bfloat16).astype(jnp.float32)
+    new_latent = rms_scale(uw_vm[:, QR : QR + rank], kv_gain_ref[...].reshape(1, rank)).astype(jnp.bfloat16)
     new_rope = rotate_wide(
         uw_vm[:, QR + rank : QR + rank + LANES], cos_wide, sin_wide, lane_at, half
     ).astype(jnp.bfloat16)
@@ -669,14 +678,6 @@
         jnp.where(local_table[None, :] == slot_at[:, None], flat_index[None, :], 0), axis=1
     )
     places = jnp.concatenate([owner, local_table])
-    half = rope_width // 2
-    lane = jnp.arange(LANES, dtype=jnp.int32)
-    freq = 10000.0 ** (-2.0 * (lane % half).astype(jnp.float32) / rope_width)
-    angles = lengths.astype(jnp.float32)[:, None] * freq[None, :]
-    inside = (lane < rope_width)[None, :]
-    cos_wide = jnp.where(inside, jnp.cos(angles), 0.0)
-    sine = jnp.sin(angles)
-    sin_wide = jnp.where(inside, jnp.where((lane < half)[None, :], -sine, sine), 0.0)
     dims = dict(
         heads=heads,
         own_heads=own_heads,
@@ -705,10 +706,10 @@
             jax.ShapeDtypeStruct((batch, heads * VD), bf16),
             jax.ShapeDtypeStruct((batch, LATENT_RANK + rope_width), bf16),
         ),
-        in_specs=[smem, smem] + [vmem] * 5 + [anywhere] * 6,
+        in_specs=[smem, smem] + [vmem] * 3 + [anywhere] * 6,
         out_specs=(vmem, vmem),
         scratch_shapes=[
-            pltpu.VMEM(united_down.shape, bf16),
+            pltpu.VMEM(united_down.shape[::-1], bf16),
             pltpu.VMEM(q_up.shape, bf16),
             pltpu.VMEM((LATENT_RANK, own_heads * NOPE), bf16),
             pltpu.VMEM((LATENT_RANK, own_heads * VD), bf16),
@@ -749,11 +750,9 @@
         places,
         lengths,
         hidden_in,
-        cos_wide,
-        sin_wide,
-        q_gain[None, :],
-        kv_gain[None, :],
-        united_down,
+        q_gain,
+        kv_gain,
+        united_down.T,
         q_up,
         key_up,
         value_up,

time: 108 us -> 96.6 us (0.89)
  local copies, waits for them, and re-layouts: 12.8 us -> 3.07 us
  other arithmetic: 2.8 us -> 1.39 us
    unnamed x3 -> x2, local copies, waits for them, and re-layouts: 11.3 us -> 2.9 us
    broadcast_in_dim x1 -> x0, local copies, waits for them, and re-layouts: 1.3 us -> none  [kernel_body(): q_gain[None, :]]
where the time goes in v2:
time: 96.6 us; the launch traced here: 96.3 us
  Pallas kernels  91.2 us (94%)
  local copies, waits for them, and re-layouts  3.07 us (3%)
  other arithmetic  1.39 us (1%)
    pallas_call x1, Pallas kernels, kernel_body(): pl.pallas_call(functools.partial(step_kernel, n_seq, n_tensor, dims), out...  91.2 us
    unnamed x2, local copies, waits for them, and re-layouts  2.9 us

profile of v2, /device:TPU:0, one launch (start us, length us, event | category | flops | bytes accessed | tf_op | source)
XLA Modules:
  0.0 96.3 jit_solution(18227821092092837600)
XLA Ops:
  0.6 0.7 broadcast_subtract_fusion
  1.3 0.1 copy.15
  1.4 0.1 sub.15
  1.5 0.1 select_reduce_fusion
  1.6 0.6 pad_add_fusion.idx_ref
  2.2 91.2 %shard_map.122 = (bf16[16,4096]{1,0:T(8,128)(2,1)}, bf16[16,576]{1,0:T(8,128)(2,1)}) custom-call(s32[128]{0:T(128)} %pad_add_fusion.idx_ref, s32[16]{0:T(128)} %len_ref.1, bf16[16,5120]{1,0:T(8,128)(2,1)} %hidden_ref.1, f32[1536]{0:T(1024)} %q_gain_ref.1, f32[512]{0:T(512)} %kv_gain_ref.1, bf16[528,5120]{1,0:T(8,128)(2,1)} %bitcast.1, ...), custom_call_target="tpu_custom_call" | custom-call | tf_op jit(solution)/shard_map/pallas_call | solution.py:703
  93.4 1.6 %copy.18 = bf16[16,4096]{1,0:T(8,128)(2,1)} copy(bf16[16,4096]{1,0:T(8,128)(2,1)} %get-tuple-element.4) | data formatting | bytes 262144
  95.0 1.3 %copy.19 = bf16[16,576]{1,0:T(8,128)(2,1)} copy(bf16[16,576]{1,0:T(8,128)(2,1)} %get-tuple-element.5) | data formatting | bytes 36864
